TPU v7x, 8 devices: a whole 2x2x1 slice. The times are simulated.
8 devices in a mesh: replica: 2 (over z, y), model: 4 (over x, core).
Axes of the slice: x: 2, y: 2, z: 1, core: 2. Of those that a mesh axis runs over, the one named last changes fastest.
Arguments:
- tokens: bfloat16 [256, 3072], P('replica'), parts along dimension 0
- lengths: int32 [256], P('replica'), parts along dimension 0
- k_cache: bfloat16 [256, 8, 512, 128], P('replica'), parts along dimension 0
- v_cache: bfloat16 [256, 8, 512, 128], P('replica'), parts along dimension 0
- norm_gain: bfloat16 [3072], replicated
- w_query: bfloat16 [3072, 3072], P(None, 'model')
- w_key: bfloat16 [3072, 1024], replicated
- w_value: bfloat16 [3072, 1024], replicated
- w_out: bfloat16 [3072, 3072], P('model')
- w_gate: bfloat16 [3072, 12288], P(None, 'model')
- w_up: bfloat16 [3072, 12288], P(None, 'model')
- w_down: bfloat16 [12288, 3072], P('model')
Outputs:
- output 1: bfloat16 [256, 3072], P('replica'), parts along dimension 0
- output 2: bfloat16 [256, 8, 128], P(('replica', 'model')), parts along dimension 0
- output 3: bfloat16 [256, 8, 128], P(('replica', 'model')), parts along dimension 0
There are 2 independent parts. A program takes and returns all parts, laid end to end along the dimension named above; an argument that names none is the same for every part.
All inputs are finite; a program needn't handle non-finite values.
Results may differ from a plain program's by a relative error of at most 0.00484794.
Values are sent between devices in bfloat16 or wider.
A program may use at most 1.5 GiB of HBM per device.

v0:
```python
import functools
import math

import jax
import jax.numpy as jnp
import numpy as np
from jax import lax
from jax.experimental import pallas as pl
from jax.experimental.pallas import tpu as pltpu
from jax.sharding import PartitionSpec as P

ROPE_BASE = 10000.0
NORM_EPS = 1e-6
MASK_VALUE = -1e30
MESH = pl.DeviceIdType.MESH
F32 = jnp.float32
BF16 = jnp.bfloat16
TILE = 256
SLOTS = 12
LAGS = (1, 6, 11, 13)
CHUNK = 64
UNROLL = 16
VMEM_BYTES = 67_043_328
RESULT_BYTES = 12_000_000
PIECES_SCORE = 12
PIECES_VALUE = 11
RING = 256


def front_kernel(lengths, tokens, gain_hbm, freq_hbm, k_cache, v_cache, w_query, w_key, w_value, w_gate, w_up,
                 packed,
                 x_buf, h_buf, w_buf, k_ring, v_ring, q_buf, kn_buf, vn_buf, fresh, score, peak, total, mixed, angle, rot,
                 gain, freq, o_out, kv_out, u_out,
                 item_seq, item_pos, out_sem, x_sem, w_sem, k_sem, v_sem):
    batch, model_dim = tokens.shape
    head_dim = freq.shape[1]
    local_kv = kv_out.shape[1] // (2 * head_dim)
    heads = o_out.shape[1] // head_dim
    ratio = heads // local_kv
    q_tiles = w_query.shape[1] // TILE
    lead = q_tiles + 2
    half = TILE // 2
    pieces = w_gate.shape[1] // half
    ring_steps = RING // UNROLL
    first_steps = batch // UNROLL
    scale = head_dim ** -0.5
    me = lax.axis_index('model')
    local = pl.ds(me * local_kv, local_kv)
    lanes = local_kv * CHUNK

    def w_copy(src, tile, t):
        return pltpu.make_async_copy(src.at[:, pl.ds(pl.multiple_of(tile * TILE, TILE), TILE)], w_buf.at[t], w_sem.at[t])

    def start_piece(p, slot):
        for n, src in enumerate((w_gate, w_up)):
            pltpu.make_async_copy(src.at[:, pl.ds(pl.multiple_of(p * half, half), half)],
                                  w_buf.at[slot, :, n * half:(n + 1) * half], w_sem.at[slot]).start()

    def first_copy(cache, ring, sem, step):
        rows = pl.ds(step * UNROLL, UNROLL)
        return pltpu.make_async_copy(cache.at[rows, local, pl.ds(0, CHUNK)], ring.at[rows], sem.at[step])

    def item_copy(cache, ring, sem, k):
        slot = lax.rem(k, RING)
        return pltpu.make_async_copy(cache.at[lax.rem(item_seq[k], batch), local, pl.ds(pl.multiple_of(item_pos[k], CHUNK), CHUNK)],
                                     ring.at[slot], sem.at[lax.div(slot, UNROLL)])

    x_copy = pltpu.make_async_copy(tokens, x_buf, x_sem.at[0])
    gain_copy = pltpu.make_async_copy(gain_hbm, gain, x_sem.at[1])
    freq_copy = pltpu.make_async_copy(freq_hbm, freq, x_sem.at[2])
    for copy in (freq_copy, x_copy, gain_copy):
        copy.start()
    lead_copies = [w_copy(w_key, me, 0), w_copy(w_value, me, 1)] + [w_copy(w_query, t, 2 + t) for t in range(q_tiles)]
    for copy in lead_copies:
        copy.start()
    for step in range(first_steps):
        first_copy(k_cache, k_ring, k_sem, step).start()
    for p in range(SLOTS - lead):
        start_piece(p, lead + p)
    for step in range(first_steps):
        first_copy(v_cache, v_ring, v_sem, step).start()

    def second(i, k):
        for r in range(UNROLL):
            seq = i * UNROLL + r
            item_seq[k] = seq
            item_pos[k] = CHUNK
            k = k + (lengths[seq] > CHUNK).astype(jnp.int32)
        return k

    begin = batch
    end = lax.fori_loop(0, batch // UNROLL, second, batch)
    for c in range(2, k_cache.shape[2] // CHUNK):
        def further(i, k):
            seq = item_seq[i]
            item_seq[k] = seq
            item_pos[k] = c * CHUNK
            return k + (lengths[seq] > c * CHUNK).astype(jnp.int32)

        begin, end = end, lax.fori_loop(begin, end, further, end)
    steps = lax.div(end + (UNROLL - 1), UNROLL)

    @pl.loop(end, steps * UNROLL)
    def _(k):
        item_seq[k] = batch
        item_pos[k] = 0

    @pl.loop(batch, jnp.minimum(steps * UNROLL, RING))
    def _(k):
        item_copy(k_cache, k_ring, k_sem, k).start()
        item_copy(v_cache, v_ring, v_sem, k).start()

    freq_copy.wait()

    @pl.loop(0, batch // 8)
    def _(i):
        for r in range(8):
            angle[pl.ds(i * 8 + r, 1), :] = lengths[i * 8 + r].astype(F32) * freq[...]

    first = lax.broadcasted_iota(jnp.int32, (batch, head_dim), 1) < head_dim // 2
    rot[0] = jnp.cos(angle[...])
    rot[1] = jnp.where(first, -jnp.sin(angle[...]), jnp.sin(angle[...]))
    q_buf[...] = jnp.zeros(q_buf.shape, F32)

    x_copy.wait()
    gain_copy.wait()
    x = x_buf[...].astype(F32)
    mean_sq = jnp.mean(x * x, axis=-1, keepdims=True)
    h_buf[...] = (x * lax.rsqrt(mean_sq + NORM_EPS) * gain[...].reshape(1, model_dim).astype(F32)).astype(BF16)

    def rope(a):
        return a * rot[0] + pltpu.roll(a, head_dim // 2, 1) * rot[1]

    for t, copy in enumerate(lead_copies):
        copy.wait()
        prod = jnp.dot(h_buf[...], w_buf[t], preferred_element_type=F32)
        if SLOTS - lead + t < pieces:
            start_piece(SLOTS - lead + t, t)
        for j in range(TILE // head_dim):
            a = prod[:, j * head_dim:(j + 1) * head_dim]
            if t >= 2:
                q_buf[:, (t - 2) * (TILE // head_dim) + j, :] = rope(a).astype(BF16).astype(F32)
            else:
                a = (rope(a) if t == 0 else a).astype(BF16)
                col = (t * local_kv + j) * head_dim
                kv_out[:, col:col + head_dim] = a
                (kn_buf, vn_buf)[t][j] = a
    width = u_out.shape[1]
    o_at, kv_at = width, width + heads * head_dim
    x_at = kv_at + kv_out.shape[1]
    kv_copy = pltpu.make_async_copy(kv_out, packed.at[:, kv_at:x_at], out_sem.at[0])
    kv_copy.start()
    quarter = batch // 4
    x_part = model_dim // 4
    x_rows = pl.ds(pl.multiple_of(me * quarter, quarter), quarter)
    x_copies = [pltpu.make_async_copy(x_buf.at[x_rows, n * x_part:(n + 1) * x_part],
                                      packed.at[n * quarter:(n + 1) * quarter, x_at:x_at + x_part], out_sem.at[3 + n]) for n in range(4)]
    for copy in x_copies:
        copy.start()
    peak[batch] = jnp.full(peak.shape[1:], MASK_VALUE, F32)
    total[batch] = jnp.zeros(total.shape[1:], F32)
    mixed[batch] = jnp.zeros(mixed.shape[1:], F32)

    sub = q_buf.shape[1]
    lane = lax.broadcasted_iota(jnp.int32, (sub, lanes), 1)
    head = lax.broadcasted_iota(jnp.int32, (sub, lanes), 0)
    own = (lax.div(lane, CHUNK) == lax.div(head, ratio)) & (head < heads)
    pos_in = jnp.where(own, lax.rem(lane, CHUNK), 1 << 20)

    line = lax.broadcasted_iota(jnp.int32, (CHUNK, sub, lanes), 0)
    mine = line == pos_in[None]
    blocks = [slice(b0, b0 + CHUNK) for b0 in range(0, batch, CHUNK)]
    for rows in blocks:
        q = q_buf[rows].reshape(CHUNK * sub, head_dim).astype(BF16)
        s = lax.dot_general(q, kn_buf[:, rows].reshape(lanes, head_dim), (((1,), (1,)), ((), ())), preferred_element_type=F32) * scale
        s = jnp.where(mine, s.reshape(CHUNK, sub, lanes), MASK_VALUE)
        fresh[rows] = s
        peak[rows] = s

    def wait_step(ring, sem, step):
        at = lax.rem(step, ring_steps)
        pltpu.make_async_copy(ring.at[pl.ds(0, UNROLL)], ring.at[pl.ds(at * UNROLL, UNROLL)], sem.at[at]).wait()

    def refill(cache, ring, sem, step):
        @pl.when(step + ring_steps < steps)
        def _():
            @pl.loop(0, UNROLL)
            def _(u):
                item_copy(cache, ring, sem, (step + ring_steps) * UNROLL + u).start()

    def item(step, u, listed):
        k = step * UNROLL + u
        if listed:
            return k, item_seq[k], lax.rem(item_seq[k], batch), item_pos[k]
        return k, k, k, 0

    def score_step(step, listed):
        base = lax.rem(step, ring_steps) * UNROLL
        found = []
        for u in range(UNROLL):
            k, seq, row, pos = item(step, u, listed)
            keys = k_ring[base + u].reshape(lanes, head_dim)
            s = lax.dot_general(q_buf[row].astype(BF16), keys, (((1,), (1,)), ((), ())), preferred_element_type=F32) * scale
            s = jnp.where(pos_in < lengths[row] - pos, s, MASK_VALUE)
            score[k] = s
            found.append((seq, s))
        for seq, s in found:
            peak[seq] = jnp.maximum(peak[seq], s)

    def value_step(step, listed):
        base = lax.rem(step, ring_steps) * UNROLL
        found = []
        for u in range(UNROLL):
            k, seq, row, pos = item(step, u, listed)
            p = jnp.exp(score[k] - peak[seq])
            values = v_ring[base + u].reshape(lanes, head_dim)
            found.append((seq, p, jnp.dot(p.astype(BF16), values, preferred_element_type=F32)))
        for seq, p, o in found:
            total[seq] = total[seq] + p
            mixed[seq] = mixed[seq] + o

    def u_copy(p):
        cols = pl.ds(pl.multiple_of(p * half, half), half)
        return pltpu.make_async_copy(u_out.at[:, cols], packed.at[:, cols], out_sem.at[1])

    def wait_piece(p):
        slot = lax.rem(lead + p, SLOTS)
        pltpu.make_async_copy(w_gate.at[:, pl.ds(0, TILE)], w_buf.at[slot], w_sem.at[slot]).wait()

    def piece(p):
        prod = jnp.dot(h_buf[...], w_buf[lax.rem(lead + p, SLOTS)], preferred_element_type=F32)
        u_out[:, pl.ds(pl.multiple_of(p * half, half), half)] = (jax.nn.silu(prod[:, :half]) * prod[:, half:]).astype(BF16)

    def after_piece(p):
        u_copy(p).start()

        @pl.when(p + SLOTS < pieces)
        def _():
            start_piece(p + SLOTS, lax.rem(lead + p, SLOTS))

    def both(attend_step, cache, ring, sem, p0, p1):
        @pl.loop(0, first_steps)
        def _(s):
            wait_step(ring, sem, s)
            wait_piece(p0 + s)
            attend_step(s, False)
            piece(p0 + s)
            refill(cache, ring, sem, s)
            after_piece(p0 + s)

        fused = jnp.minimum(steps, p1 - p0)

        @pl.loop(first_steps, fused)
        def _(s):
            wait_step(ring, sem, s)
            wait_piece(p0 + s)
            attend_step(s, True)
            piece(p0 + s)
            refill(cache, ring, sem, s)
            after_piece(p0 + s)

        @pl.loop(fused, steps)
        def _(s):
            wait_step(ring, sem, s)
            attend_step(s, True)
            refill(cache, ring, sem, s)

        return p0 + fused

    reached = both(score_step, k_cache, k_ring, k_sem, 0, PIECES_SCORE)

    @pl.loop(reached, PIECES_SCORE)
    def _(p):
        wait_piece(p)
        piece(p)
        after_piece(p)

    for rows in blocks:
        top = jnp.broadcast_to(jnp.max(peak[rows], axis=-1, keepdims=True), (CHUNK, sub, lanes))
        peak[rows] = top
        p = jnp.exp(fresh[rows] - top)
        total[rows] = p
        o = jnp.dot(p.reshape(CHUNK * sub, lanes).astype(BF16), vn_buf[:, rows].reshape(lanes, head_dim), preferred_element_type=F32)
        mixed[rows] = o.reshape(CHUNK, sub, head_dim)

    reached = both(value_step, v_cache, v_ring, v_sem, PIECES_SCORE, PIECES_SCORE + PIECES_VALUE)

    q_buf[...] = mixed[:batch] / jnp.sum(total[:batch], axis=-1, keepdims=True)
    for h in range(heads):
        o_out[:, h * head_dim:(h + 1) * head_dim] = q_buf[:, h, :].astype(BF16)
    o_copy = pltpu.make_async_copy(o_out, packed.at[:, o_at:kv_at], out_sem.at[2])
    o_copy.start()

    @pl.loop(reached, pieces)
    def _(p):
        wait_piece(p)
        piece(p)
        after_piece(p)

    kv_copy.wait()
    o_copy.wait()
    for copy in x_copies:
        copy.wait()
    pltpu.make_async_copy(u_out, packed.at[:, :width], out_sem.at[1]).wait()


def front(tokens, lengths, k_cache, v_cache, norm_gain, w_query, w_key, w_value, w_gate, w_up, groups):
    batch, model_dim = tokens.shape
    kv_heads, context, head_dim = k_cache.shape[1:]
    local_kv = kv_heads // groups
    q_dim = w_query.shape[1]
    width = w_gate.shape[1]
    half_freq = np.exp(np.arange(head_dim // 2) * (-2.0 * math.log(ROPE_BASE) / head_dim))
    freq = jnp.asarray(np.concatenate([half_freq, half_freq])[None, :], F32)
    items = batch * (context // CHUNK) + UNROLL
    lanes = local_kv * CHUNK
    dma = pltpu.SemaphoreType.DMA
    hbm = pl.BlockSpec(memory_space=pltpu.HBM)
    smem = pl.BlockSpec(memory_space=pltpu.SMEM)
    return pl.pallas_call(
        front_kernel,
        out_shape=jax.ShapeDtypeStruct((batch, width + q_dim + 2 * local_kv * head_dim + model_dim // 4), BF16),
        in_specs=[smem] + [hbm] * 10,
        out_specs=hbm,
        scratch_shapes=[
            pltpu.VMEM((batch, model_dim), BF16),
            pltpu.VMEM((batch, model_dim), BF16),
            pltpu.VMEM((SLOTS, model_dim, TILE), BF16),
            pltpu.VMEM((RING, local_kv, CHUNK, head_dim), BF16),
            pltpu.VMEM((RING, local_kv, CHUNK, head_dim), BF16),
            pltpu.VMEM((batch, 8, head_dim), F32),
            pltpu.VMEM((local_kv, batch, head_dim), BF16),
            pltpu.VMEM((local_kv, batch, head_dim), BF16),
            pltpu.VMEM((batch, 8, lanes), F32),
            pltpu.VMEM((items, 8, lanes), F32),
            pltpu.VMEM((batch + 1, 8, lanes), F32),
            pltpu.VMEM((batch + 1, 8, lanes), F32),
            pltpu.VMEM((batch + 1, 8, head_dim), F32),
            pltpu.VMEM((batch, head_dim), F32),
            pltpu.VMEM((2, batch, head_dim), F32),
            pltpu.VMEM((model_dim,), BF16),
            pltpu.VMEM((1, head_dim), F32),
            pltpu.VMEM((batch, q_dim), BF16),
            pltpu.VMEM((batch, 2 * local_kv * head_dim), BF16),
            pltpu.VMEM((batch, width), BF16),
            pltpu.SMEM((items,), jnp.int32),
            pltpu.SMEM((items,), jnp.int32),
            dma((7,)), dma((3,)), dma((SLOTS,)), dma((RING // UNROLL,)), dma((RING // UNROLL,)),
        ],
        compiler_params=pltpu.CompilerParams(vmem_limit_bytes=VMEM_BYTES),
        name="front",
    )(lengths, tokens, norm_gain, freq, k_cache, v_cache, w_query, w_key, w_value, w_gate, w_up)


def back_kernel(packed, w_down, w_out,
                y_out, key_out, value_out, _,
                u_buf, o_buf, kv_buf, x_buf, w_buf, wo_buf, part, from_sib, to_cross, from_cross, y_buf, kv_in, head_buf,
                in_sem, w_sem, wo_sem, kv_send, kv_recv, s1_send, s1_recv, s2_send, s2_recv,
                yc_send, yc_recv, ys_send, ys_recv, yr_send, yr_recv):
    me = lax.axis_index('model')
    core = lax.rem(me, 2)
    chip = lax.div(me, 2)
    sib = chip * 2 + (1 - core)
    cross = (1 - chip) * 2 + core
    diag = (1 - chip) * 2 + (1 - core)
    n_out = w_down.shape[1] // TILE
    head_dim = head_buf.shape[2]
    local_kv = kv_buf.shape[2] // (2 * head_dim)
    lag_sib, lag_cross, lag_relay, lag_store = LAGS

    barrier = pltpu.get_barrier_semaphore()
    for peer in (sib, cross, diag):
        pl.semaphore_signal(barrier, inc=1, device_id={'model': peer}, device_id_type=MESH)

    def cols(tile):
        return pl.ds(pl.multiple_of(tile * TILE, TILE), TILE)

    def down_copy(c):
        return pltpu.make_async_copy(w_down.at[:, cols(c)], w_buf.at[c], w_sem.at[c])

    def remote(src, dst, send, recv, peer):
        return pltpu.make_async_remote_copy(src_ref=src, dst_ref=dst, send_sem=send, recv_sem=recv,
                                            device_id={'model': peer}, device_id_type=MESH)

    def out_copy(c):
        return pltpu.make_async_copy(w_out.at[:, cols(c)], wo_buf.at[c], wo_sem.at[c])

    devices, rows = kv_buf.shape[:2]
    width, q_dim = u_buf.shape[1], o_buf.shape[1]
    kv_at = width + q_dim
    x_at = kv_at + kv_buf.shape[2]
    x_part = x_buf.shape[2]
    o_copy = pltpu.make_async_copy(packed.at[:, width:kv_at], o_buf, in_sem.at[0])
    u_copy = pltpu.make_async_copy(packed.at[:, :width], u_buf, in_sem.at[1])
    kv_copies = [pltpu.make_async_copy(packed.at[n * rows:(n + 1) * rows, kv_at:x_at], kv_buf.at[n], in_sem.at[2 + n]) for n in range(devices)]
    x_copies = [pltpu.make_async_copy(packed.at[n * rows:(n + 1) * rows, x_at:x_at + x_part], x_buf.at[n], in_sem.at[2 + devices + n])
                for n in range(devices)]
    for copy in (o_copy, u_copy, out_copy(0), down_copy(0), *kv_copies, *x_copies):
        copy.start()

    @pl.loop(1, n_out)
    def _(c):
        out_copy(c).start()
        down_copy(c).start()

    for copy in kv_copies:
        copy.wait()
    pl.semaphore_wait(barrier, 3)
    kv_sends = []
    for n, peer in enumerate((sib, cross, diag)):
        send = remote(kv_buf.at[peer], kv_in.at[me], kv_send.at[n], kv_recv.at[n], peer)
        send.start()
        kv_sends.append(send)
    for copy in (o_copy, u_copy, *x_copies):
        copy.wait()

    def sib_send(c):
        return remote(part.at[c, :, 1 - core], from_sib.at[c], s1_send.at[c], s1_recv.at[c], sib)

    def cross_send(c):
        return remote(to_cross.at[c], from_cross.at[c], s2_send.at[c], s2_recv.at[c], cross)

    def y_cross(c):
        return remote(y_buf.at[c, me], y_buf.at[c, me], yc_send.at[c], yc_recv.at[c], cross)

    def y_sib(c):
        return remote(y_buf.at[c, me], y_buf.at[c, me], ys_send.at[c], ys_recv.at[c], sib)

    def y_relay(c):
        return remote(y_buf.at[c, cross], y_buf.at[c, cross], yr_send.at[c], yr_recv.at[c], sib)

    @pl.loop(0, n_out + lag_store)
    def _(i):
        @pl.when(i < n_out)
        def _():
            out_copy(i).wait()
            total = jnp.dot(o_buf[...], wo_buf[i], preferred_element_type=F32)
            down_copy(i).wait()
            total += jnp.dot(u_buf[...], w_buf[i], preferred_element_type=F32)
            part[i] = total.reshape(part.shape[1:])
            sib_send(i).start()

        @pl.when((i >= lag_sib) & (i < n_out + lag_sib))
        def _():
            c = i - lag_sib
            sib_send(c).wait_recv()
            to_cross[c] = part[c, 1 - chip, core] + from_sib[c, 1 - chip]
            cross_send(c).start()

        @pl.when((i >= lag_cross) & (i < n_out + lag_cross))
        def _():
            c = i - lag_cross
            cross_send(c).wait_recv()
            total = part[c, chip, core] + from_sib[c, chip] + from_cross[c]
            x = x_buf[lax.div(c * TILE, x_part), :, pl.ds(pl.multiple_of(lax.rem(c * TILE, x_part), TILE), TILE)]
            y_buf[c, me] = (x.astype(F32) + total).astype(BF16)
            y_cross(c).start()
            y_sib(c).start()

        @pl.when((i >= lag_relay) & (i < n_out + lag_relay))
        def _():
            c = i - lag_relay
            y_cross(c).wait_recv()
            y_relay(c).start()

        @pl.when(i == n_out)
        def _():
            for send in kv_sends:
                send.wait_recv()
            kv_in[me] = kv_buf[me]
            for half, out in enumerate((key_out, value_out)):
                for source in range(kv_in.shape[0]):
                    for g in range(local_kv):
                        start = (half * local_kv + g) * head_dim
                        head_buf[:, source * local_kv + g, :] = kv_in[source, :, start:start + head_dim].astype(F32)
                out[...] = head_buf[...].astype(BF16)

        @pl.when(i >= lag_store)
        def _():
            c = i - lag_store
            y_sib(c).wait_recv()
            y_relay(c).wait_recv()
            y_out[:, :, cols(c)] = y_buf[c]

    for send in kv_sends:
        send.wait_send()

    @pl.loop(0, n_out)
    def _(c):
        sib_send(c).wait_send()
        cross_send(c).wait_send()
        y_cross(c).wait_send()
        y_sib(c).wait_send()
        y_relay(c).wait_send()


def back(packed, w_down, w_out, kv_heads, head_dim, devices):
    batch = packed.shape[0]
    width, model_dim = w_down.shape
    q_dim = w_out.shape[0]
    rows = batch // devices
    n_out = model_dim // TILE
    kv_width = 2 * (kv_heads // devices) * head_dim
    dma = pltpu.SemaphoreType.DMA
    hbm = pl.BlockSpec(memory_space=pltpu.HBM)
    vmem = pl.BlockSpec(memory_space=pltpu.VMEM)
    y, key_out, value_out, _ = pl.pallas_call(
        back_kernel,
        out_shape=(jax.ShapeDtypeStruct((devices, rows, model_dim), BF16),
                   jax.ShapeDtypeStruct((rows, kv_heads, head_dim), BF16),
                   jax.ShapeDtypeStruct((rows, kv_heads, head_dim), BF16),
                   jax.ShapeDtypeStruct(packed.shape, BF16)),
        in_specs=[hbm] * 3,
        out_specs=(vmem, vmem, vmem, hbm),
        input_output_aliases={0: 3},
        scratch_shapes=[
            pltpu.VMEM((batch, width), BF16),
            pltpu.VMEM((batch, q_dim), BF16),
            pltpu.VMEM((devices, rows, kv_width), BF16),
            pltpu.VMEM((4, rows, model_dim // 4), BF16),
            pltpu.VMEM((n_out, width, TILE), BF16),
            pltpu.VMEM((n_out, q_dim, TILE), BF16),
            pltpu.VMEM((n_out, 2, 2, rows, TILE), F32),
            pltpu.VMEM((n_out, 2, rows, TILE), F32),
            pltpu.VMEM((n_out, rows, TILE), F32),
            pltpu.VMEM((n_out, rows, TILE), F32),
            pltpu.VMEM((n_out, devices, rows, TILE), BF16),
            pltpu.VMEM((devices, rows, kv_width), BF16),
            pltpu.VMEM((rows, kv_heads, head_dim), F32),
            dma((2 + 2 * devices,)), dma((n_out,)), dma((n_out,)), dma((3,)), dma((3,)),
        ] + [dma((n_out,))] * 10,
        compiler_params=pltpu.CompilerParams(collective_id=0, has_side_effects=True, vmem_limit_bytes=VMEM_BYTES - RESULT_BYTES),
        name="back",
    )(packed, w_down, w_out)
    return finish(y.reshape(batch, model_dim), key_out, value_out)


def finish_kernel(*refs):
    half = (len(refs) - 1) // 2
    copies = [pltpu.make_async_copy(refs[n], refs[half + n], refs[-1].at[n]) for n in range(half)]
    for copy in copies:
        copy.start()
    for copy in copies:
        copy.wait()


def finish(*arrays):
    return pl.pallas_call(
        finish_kernel,
        out_shape=tuple(jax.ShapeDtypeStruct(a.shape, a.dtype) for a in arrays),
        in_specs=[pl.BlockSpec(memory_space=pltpu.VMEM)] * len(arrays),
        out_specs=tuple(pl.BlockSpec(memory_space=pltpu.HBM) for _ in arrays),
        scratch_shapes=[pltpu.SemaphoreType.DMA((len(arrays),))],
        compiler_params=pltpu.CompilerParams(vmem_limit_bytes=4 * 2 ** 20),
        name="finish",
    )(*arrays)


def solution(mesh):
    groups = mesh.shape['model']

    def local_step(tokens, lengths, k_cache, v_cache, norm_gain, w_query, w_key, w_value, w_out, w_gate, w_up, w_down):
        kv_heads, _, head_dim = k_cache.shape[1:]
        packed = front(tokens, lengths, k_cache, v_cache, norm_gain, w_query, w_key, w_value, w_gate, w_up, groups)
        return back(packed, w_down, w_out, kv_heads, head_dim, groups)

    in_specs = (P('replica', None), P('replica'), P('replica', None, None, None), P('replica', None, None, None), P(None), P(None, 'model'), P(None, None), P(None, None), P('model', None), P(None, 'model'), P(None, 'model'), P('model', None))
    out_specs = (P('replica', None), P(('replica', 'model'), None, None), P(('replica', 'model'), None, None))
    return jax.shard_map(local_step, mesh=mesh, in_specs=in_specs, out_specs=out_specs, check_vma=False)
```

profile of v0, /device:TPU:0, one launch (start us, length us, event | category | flops | bytes accessed | tf_op | source)
XLA Modules:
  0.0 49.9 jit_solution(8361653998171671100)
XLA Ops:
  0.6 25.1 %front.1.packed = bf16[128,5120]{1,0:T(8,128)(2,1)} custom-call(s32[128]{0:T(128)} %lengths.1, bf16[128,3072]{1,0:T(8,128)(2,1)} %tokens.1, bf16[3072]{0:T(1024)(128)(2,1)} %gain_hbm.1, f32[1,128]{1,0:T(1,128)} %constant.2.clone.freq_hbm, bf16[128,8,512,128]{3,2,1,0:T(8,128)(2,1)} %k_cache.1, bf16[128,8,512,128]{3,2,1,0:T(8,128)(2,1)} %v_cache.1, ...), custom_call_target="tpu_custom_call" | custom-call | tf_op jit(solution)/shard_map/front/pallas_call | solution.py:320
  25.8 23.2 %back.1 = (bf16[4,32,3072]{2,1,0:T(8,128)(2,1)S(1)}, bf16[32,8,128]{2,1,0:T(8,128)(2,1)S(1)}, bf16[32,8,128]{2,1,0:T(8,128)(2,1)S(1)}, bf16[128,5120]{1,0:T(8,128)(2,1)}) custom-call(bf16[128,5120]{1,0:T(8,128)(2,1)} %front.1.packed, bf16[3072,3072]{1,0:T(8,128)(2,1)} %w_down.1, bf16[768,3072]{1,0:T(8,128)(2,1)} %w_out.1), custom_call_target="tpu_custom_call", output_to_operand_aliasing={{3}: (0, {})} | custom-call | tf_op jit(solution)/shard_map/back/pallas_call | solution.py:507
  49.0 0.9 %finish.1 = (bf16[128,3072]{1,0:T(8,128)(2,1)}, bf16[32,8,128]{2,1,0:T(8,128)(2,1)}, bf16[32,8,128]{2,1,0:T(8,128)(2,1)}) custom-call(bf16[128,3072]{1,0:T(8,128)(2,1)S(1)} %bitcast.1, bf16[32,8,128]{2,1,0:T(8,128)(2,1)S(1)} %get-tuple-element.7.refs_1_, bf16[32,8,128]{2,1,0:T(8,128)(2,1)S(1)} %get-tuple-element.8.refs_2_), custom_call_target="tpu_custom_call" | custom-call | tf_op jit(solution)/shard_map/finish/pallas_call | solution.py:548
where the time goes:
time: 50.6 us; the launch traced here: 49.9 us
  Pallas kernels  49.3 us (97%)
  between operations  0.65 us (1%)
    pallas_call x1, Pallas kernels, front(): pl.pallas_call(front_kernel, out_shape=jax.ShapeDtypeStruct((batch, width...  25.1 us
    pallas_call x1, Pallas kernels, back(): pl.pallas_call(back_kernel, out_shape=(jax.ShapeDtypeStruct((devices, row...  23.2 us

commit v1 on v0

--- a/solution.py
+++ b/solution.py
@@ -403,41 +403,49 @@
         out_copy(c).start()
         down_copy(c).start()
 
-    for copy in kv_copies:
+    for copy in (o_copy, u_copy):
+        copy.wait()
+
+    kv_peers = (sib, cross, diag)
+
+    def kv_copy(n):
+        return remote(kv_buf.at[kv_peers[n]], kv_in.at[me], kv_send.at[n], kv_recv.at[n], kv_peers[n])
+
+    def sib_send(c):
+        return remote(part.at[c, :, 1 - core], from_sib.at[c], s1_send, s1_recv.at[c], sib)
+
+    def cross_send(c):
+        return remote(to_cross.at[c], from_cross.at[c], s2_send, s2_recv.at[c], cross)
+
+    def y_cross(c):
+        return remote(y_buf.at[c, me], y_buf.at[c, me], yc_send, yc_recv.at[c], cross)
+
+    def y_sib(c):
+        return remote(y_buf.at[c, me], y_buf.at[c, me], ys_send, ys_recv.at[c], sib)
+
+    def y_relay(c):
+        return remote(y_buf.at[c, cross], y_buf.at[c, cross], yr_send, yr_recv.at[c], sib)
+
+    def product(c):
+        out_copy(c).wait()
+        total = jnp.dot(o_buf[...], wo_buf[c], preferred_element_type=F32)
+        down_copy(c).wait()
+        total += jnp.dot(u_buf[...], w_buf[c], preferred_element_type=F32)
+        part[c] = total.reshape(part.shape[1:])
+
+    product(0)
+    for copy in (*kv_copies, *x_copies):
         copy.wait()
     pl.semaphore_wait(barrier, 3)
-    kv_sends = []
-    for n, peer in enumerate((sib, cross, diag)):
-        send = remote(kv_buf.at[peer], kv_in.at[me], kv_send.at[n], kv_recv.at[n], peer)
-        send.start()
-        kv_sends.append(send)
-    for copy in (o_copy, u_copy, *x_copies):
-        copy.wait()
-
-    def sib_send(c):
-        return remote(part.at[c, :, 1 - core], from_sib.at[c], s1_send.at[c], s1_recv.at[c], sib)
-
-    def cross_send(c):
-        return remote(to_cross.at[c], from_cross.at[c], s2_send.at[c], s2_recv.at[c], cross)
-
-    def y_cross(c):
-        return remote(y_buf.at[c, me], y_buf.at[c, me], yc_send.at[c], yc_recv.at[c], cross)
-
-    def y_sib(c):
-        return remote(y_buf.at[c, me], y_buf.at[c, me], ys_send.at[c], ys_recv.at[c], sib)
-
-    def y_relay(c):
-        return remote(y_buf.at[c, cross], y_buf.at[c, cross], yr_send.at[c], yr_recv.at[c], sib)
-
-    @pl.loop(0, n_out + lag_store)
+    sib_send(0).start()
+    for n in range(3):
+        kv_copy(n).start()
+
+    @pl.loop(1, n_out + lag_store)
     def _(i):
         @pl.when(i < n_out)
         def _():
-            out_copy(i).wait()
-            total = jnp.dot(o_buf[...], wo_buf[i], preferred_element_type=F32)
-            down_copy(i).wait()
-            total += jnp.dot(u_buf[...], w_buf[i], preferred_element_type=F32)
-            part[i] = total.reshape(part.shape[1:])
+            product(i)
             sib_send(i).start()
 
         @pl.when((i >= lag_sib) & (i < n_out + lag_sib))
@@ -465,8 +473,8 @@
 
         @pl.when(i == n_out)
         def _():
-            for send in kv_sends:
-                send.wait_recv()
+            for n in range(3):
+                kv_copy(n).wait_recv()
             kv_in[me] = kv_buf[me]
             for half, out in enumerate((key_out, value_out)):
                 for source in range(kv_in.shape[0]):
@@ -482,16 +490,12 @@
             y_relay(c).wait_recv()
             y_out[:, :, cols(c)] = y_buf[c]
 
-    for send in kv_sends:
-        send.wait_send()
-
-    @pl.loop(0, n_out)
-    def _(c):
-        sib_send(c).wait_send()
-        cross_send(c).wait_send()
-        y_cross(c).wait_send()
-        y_sib(c).wait_send()
-        y_relay(c).wait_send()
+    for n in range(3):
+        kv_copy(n).wait_send()
+    remote(part.at[:, :, 0], from_sib, s1_send, s1_recv.at[0], sib).wait_send()
+    remote(to_cross, from_cross, s2_send, s2_recv.at[0], cross).wait_send()
+    for sem in (yc_send, ys_send, yr_send):
+        remote(y_buf.at[:, 0], y_buf.at[:, 0], sem, yc_recv.at[0], sib).wait_send()
 
 
 def back(packed, w_down, w_out, kv_heads, head_dim, devices):
@@ -528,7 +532,7 @@
             pltpu.VMEM((devices, rows, kv_width), BF16),
             pltpu.VMEM((rows, kv_heads, head_dim), F32),
             dma((2 + 2 * devices,)), dma((n_out,)), dma((n_out,)), dma((3,)), dma((3,)),
-        ] + [dma((n_out,))] * 10,
+        ] + [dma, dma((n_out,))] * 5,
         compiler_params=pltpu.CompilerParams(collective_id=0, has_side_effects=True, vmem_limit_bytes=VMEM_BYTES - RESULT_BYTES),
         name="back",
     )(packed, w_down, w_out)

time: 50.6 us -> 49.4 us (0.976); the launches traced: 49.9 us -> 49.3 us
  Pallas kernels: 49.3 us -> 48.7 us
    pallas_call x1, Pallas kernels: 23.2 us -> 22.6 us  [back(): pl.pallas_call(back_kernel, out_shape=(jax.ShapeDtypeStruct((devices, row...]
where the time goes in v1:
time: 49.4 us; the launch traced here: 49.3 us
  Pallas kernels  48.7 us (99%)
  between operations  0.65 us (1%)
    pallas_call x1, Pallas kernels, front(): pl.pallas_call(front_kernel, out_shape=jax.ShapeDtypeStruct((batch, width...  25.1 us
    pallas_call x1, Pallas kernels, back(): pl.pallas_call(back_kernel, out_shape=(jax.ShapeDtypeStruct((devices, row...  22.6 us

profile of v1, /device:TPU:0, one launch (start us, length us, event | category | flops | bytes accessed | tf_op | source)
XLA Modules:
  0.0 49.3 jit_solution(10785010907798463578)
XLA Ops:
  0.6 25.1 %front.1.packed = bf16[128,5120]{1,0:T(8,128)(2,1)} custom-call(s32[128]{0:T(128)} %lengths.1, bf16[128,3072]{1,0:T(8,128)(2,1)} %tokens.1, bf16[3072]{0:T(1024)(128)(2,1)} %gain_hbm.1, f32[1,128]{1,0:T(1,128)} %constant.2.clone.freq_hbm, bf16[128,8,512,128]{3,2,1,0:T(8,128)(2,1)} %k_cache.1, bf16[128,8,512,128]{3,2,1,0:T(8,128)(2,1)} %v_cache.1, ...), custom_call_target="tpu_custom_call" | custom-call | tf_op jit(solution)/shard_map/front/pallas_call | solution.py:320
  25.8 22.6 %back.1 = (bf16[4,32,3072]{2,1,0:T(8,128)(2,1)S(1)}, bf16[32,8,128]{2,1,0:T(8,128)(2,1)S(1)}, bf16[32,8,128]{2,1,0:T(8,128)(2,1)S(1)}, bf16[128,5120]{1,0:T(8,128)(2,1)}) custom-call(bf16[128,5120]{1,0:T(8,128)(2,1)} %front.1.packed, bf16[3072,3072]{1,0:T(8,128)(2,1)} %w_down.1, bf16[768,3072]{1,0:T(8,128)(2,1)} %w_out.1), custom_call_target="tpu_custom_call", output_to_operand_aliasing={{3}: (0, {})} | custom-call | tf_op jit(solution)/shard_map/back/pallas_call | solution.py:511
  48.4 0.9 %finish.1 = (bf16[128,3072]{1,0:T(8,128)(2,1)}, bf16[32,8,128]{2,1,0:T(8,128)(2,1)}, bf16[32,8,128]{2,1,0:T(8,128)(2,1)}) custom-call(bf16[128,3072]{1,0:T(8,128)(2,1)S(1)} %bitcast.1, bf16[32,8,128]{2,1,0:T(8,128)(2,1)S(1)} %get-tuple-element.7.refs_1_, bf16[32,8,128]{2,1,0:T(8,128)(2,1)S(1)} %get-tuple-element.8.refs_2_), custom_call_target="tpu_custom_call" | custom-call | tf_op jit(solution)/shard_map/finish/pallas_call | solution.py:552

commit v2 on v1

--- a/solution.py
+++ b/solution.py
@@ -16,22 +16,24 @@
 F32 = jnp.float32
 BF16 = jnp.bfloat16
 TILE = 256
-SLOTS = 12
+SLOTS = 8
+LEAD_NOW = 2
+PIECES_NOW = 1
 LAGS = (1, 6, 11, 13)
 CHUNK = 64
 UNROLL = 16
 VMEM_BYTES = 67_043_328
 RESULT_BYTES = 12_000_000
-PIECES_SCORE = 12
+PIECES_SCORE = 13
 PIECES_VALUE = 11
-RING = 256
+RING = 128
 
 
 def front_kernel(lengths, tokens, gain_hbm, freq_hbm, k_cache, v_cache, w_query, w_key, w_value, w_gate, w_up,
                  packed,
-                 x_buf, h_buf, w_buf, k_ring, v_ring, q_buf, kn_buf, vn_buf, fresh, score, peak, total, mixed, angle, rot,
+                 x_buf, h_buf, w_buf, k_first, v_first, k_more, v_more, q_buf, kn_buf, vn_buf, fresh, score, peak, total, mixed, angle, rot,
                  gain, freq, o_out, kv_out, u_out,
-                 item_seq, item_pos, out_sem, x_sem, w_sem, k_sem, v_sem):
+                 item_seq, item_pos, out_sem, x_sem, w_sem, kf_sem, vf_sem, km_sem, vm_sem):
     batch, model_dim = tokens.shape
     head_dim = freq.shape[1]
     local_kv = kv_out.shape[1] // (2 * head_dim)
@@ -56,14 +58,16 @@
             pltpu.make_async_copy(src.at[:, pl.ds(pl.multiple_of(p * half, half), half)],
                                   w_buf.at[slot, :, n * half:(n + 1) * half], w_sem.at[slot]).start()
 
-    def first_copy(cache, ring, sem, step):
+    def first_copy(cache, first, sem, step):
         rows = pl.ds(step * UNROLL, UNROLL)
-        return pltpu.make_async_copy(cache.at[rows, local, pl.ds(0, CHUNK)], ring.at[rows], sem.at[step])
-
-    def item_copy(cache, ring, sem, k):
-        slot = lax.rem(k, RING)
-        return pltpu.make_async_copy(cache.at[lax.rem(item_seq[k], batch), local, pl.ds(pl.multiple_of(item_pos[k], CHUNK), CHUNK)],
-                                     ring.at[slot], sem.at[lax.div(slot, UNROLL)])
+        return pltpu.make_async_copy(cache.at[rows, local, pl.ds(0, CHUNK)], first.at[rows], sem.at[step])
+
+    def start_items(cache, more, sem, step):
+        at = lax.rem(step, ring_steps)
+        for u in range(UNROLL):
+            k = step * UNROLL + u
+            pltpu.make_async_copy(cache.at[lax.rem(item_seq[k], batch), local, pl.ds(pl.multiple_of(item_pos[k], CHUNK), CHUNK)],
+                                  more.at[at * UNROLL + u], sem.at[at]).start()
 
     x_copy = pltpu.make_async_copy(tokens, x_buf, x_sem.at[0])
     gain_copy = pltpu.make_async_copy(gain_hbm, gain, x_sem.at[1])
@@ -71,14 +75,8 @@
     for copy in (freq_copy, x_copy, gain_copy):
         copy.start()
     lead_copies = [w_copy(w_key, me, 0), w_copy(w_value, me, 1)] + [w_copy(w_query, t, 2 + t) for t in range(q_tiles)]
-    for copy in lead_copies:
+    for copy in lead_copies[:LEAD_NOW]:
         copy.start()
-    for step in range(first_steps):
-        first_copy(k_cache, k_ring, k_sem, step).start()
-    for p in range(SLOTS - lead):
-        start_piece(p, lead + p)
-    for step in range(first_steps):
-        first_copy(v_cache, v_ring, v_sem, step).start()
 
     def second(i, k):
         for r in range(UNROLL):
@@ -88,28 +86,28 @@
             k = k + (lengths[seq] > CHUNK).astype(jnp.int32)
         return k
 
-    begin = batch
-    end = lax.fori_loop(0, batch // UNROLL, second, batch)
+    begin, end = 0, lax.fori_loop(0, batch // UNROLL, second, 0)
     for c in range(2, k_cache.shape[2] // CHUNK):
         def further(i, k):
-            seq = item_seq[i]
-            item_seq[k] = seq
-            item_pos[k] = c * CHUNK
-            return k + (lengths[seq] > c * CHUNK).astype(jnp.int32)
-
-        begin, end = end, lax.fori_loop(begin, end, further, end)
+            for r in range(4):
+                at = begin + i * 4 + r
+                seq = lax.rem(jnp.maximum(item_seq[at], 0), batch)
+                item_seq[k] = seq
+                item_pos[k] = c * CHUNK
+                k = k + ((lengths[seq] > c * CHUNK) & (at < end)).astype(jnp.int32)
+            return k
+
+        begin, end = end, lax.fori_loop(0, lax.div(end - begin + 3, 4), further, end)
     steps = lax.div(end + (UNROLL - 1), UNROLL)
 
-    @pl.loop(end, steps * UNROLL)
-    def _(k):
-        item_seq[k] = batch
-        item_pos[k] = 0
-
-    @pl.loop(batch, jnp.minimum(steps * UNROLL, RING))
-    def _(k):
-        item_copy(k_cache, k_ring, k_sem, k).start()
-        item_copy(v_cache, v_ring, v_sem, k).start()
-
+    for u in range(UNROLL):
+        item_seq[end + u] = batch
+        item_pos[end + u] = 0
+
+    for copy in lead_copies[LEAD_NOW:]:
+        copy.start()
+    for step in range(first_steps):
+        first_copy(k_cache, k_first, kf_sem, step).start()
     freq_copy.wait()
 
     @pl.loop(0, batch // 8)
@@ -124,6 +122,8 @@
 
     x_copy.wait()
     gain_copy.wait()
+    for p in range(PIECES_NOW):
+        start_piece(p, lead + p)
     x = x_buf[...].astype(F32)
     mean_sq = jnp.mean(x * x, axis=-1, keepdims=True)
     h_buf[...] = (x * lax.rsqrt(mean_sq + NORM_EPS) * gain[...].reshape(1, model_dim).astype(F32)).astype(BF16)
@@ -134,8 +134,13 @@
     for t, copy in enumerate(lead_copies):
         copy.wait()
         prod = jnp.dot(h_buf[...], w_buf[t], preferred_element_type=F32)
-        if SLOTS - lead + t < pieces:
-            start_piece(SLOTS - lead + t, t)
+        if t == 0:
+            for p in range(PIECES_NOW, SLOTS - lead):
+                start_piece(p, lead + p)
+        if t == 4:
+            for step in range(first_steps):
+                first_copy(v_cache, v_first, vf_sem, step).start()
+        start_piece(SLOTS - lead + t, t)
         for j in range(TILE // head_dim):
             a = prod[:, j * head_dim:(j + 1) * head_dim]
             if t >= 2:
@@ -177,29 +182,30 @@
         fresh[rows] = s
         peak[rows] = s
 
-    def wait_step(ring, sem, step):
+    def wait_first(first, sem, step):
+        pltpu.make_async_copy(first.at[pl.ds(0, UNROLL)], first.at[pl.ds(step * UNROLL, UNROLL)], sem.at[step]).wait()
+
+    def wait_more(more, sem, step):
         at = lax.rem(step, ring_steps)
-        pltpu.make_async_copy(ring.at[pl.ds(0, UNROLL)], ring.at[pl.ds(at * UNROLL, UNROLL)], sem.at[at]).wait()
-
-    def refill(cache, ring, sem, step):
+        pltpu.make_async_copy(more.at[pl.ds(0, UNROLL)], more.at[pl.ds(at * UNROLL, UNROLL)], sem.at[at]).wait()
+
+    def refill(cache, more, sem, step):
         @pl.when(step + ring_steps < steps)
         def _():
-            @pl.loop(0, UNROLL)
-            def _(u):
-                item_copy(cache, ring, sem, (step + ring_steps) * UNROLL + u).start()
+            start_items(cache, more, sem, step + ring_steps)
 
     def item(step, u, listed):
         k = step * UNROLL + u
         if listed:
-            return k, item_seq[k], lax.rem(item_seq[k], batch), item_pos[k]
-        return k, k, k, 0
+            return batch + k, lax.rem(step, ring_steps) * UNROLL + u, item_seq[k], lax.rem(item_seq[k], batch), item_pos[k]
+        return k, k, k, k, 0
 
     def score_step(step, listed):
-        base = lax.rem(step, ring_steps) * UNROLL
+        ring = k_more if listed else k_first
         found = []
         for u in range(UNROLL):
-            k, seq, row, pos = item(step, u, listed)
-            keys = k_ring[base + u].reshape(lanes, head_dim)
+            k, at, seq, row, pos = item(step, u, listed)
+            keys = ring[at].reshape(lanes, head_dim)
             s = lax.dot_general(q_buf[row].astype(BF16), keys, (((1,), (1,)), ((), ())), preferred_element_type=F32) * scale
             s = jnp.where(pos_in < lengths[row] - pos, s, MASK_VALUE)
             score[k] = s
@@ -208,12 +214,12 @@
             peak[seq] = jnp.maximum(peak[seq], s)
 
     def value_step(step, listed):
-        base = lax.rem(step, ring_steps) * UNROLL
+        ring = v_more if listed else v_first
         found = []
         for u in range(UNROLL):
-            k, seq, row, pos = item(step, u, listed)
+            k, at, seq, row, pos = item(step, u, listed)
             p = jnp.exp(score[k] - peak[seq])
-            values = v_ring[base + u].reshape(lanes, head_dim)
+            values = ring[at].reshape(lanes, head_dim)
             found.append((seq, p, jnp.dot(p.astype(BF16), values, preferred_element_type=F32)))
         for seq, p, o in found:
             total[seq] = total[seq] + p
@@ -238,36 +244,45 @@
         def _():
             start_piece(p + SLOTS, lax.rem(lead + p, SLOTS))
 
-    def both(attend_step, cache, ring, sem, p0, p1):
-        @pl.loop(0, first_steps)
-        def _(s):
-            wait_step(ring, sem, s)
+    def both(attend_step, cache, first, first_sem, more, more_sem, p0, p1):
+        fetching = jnp.minimum(steps, first_steps)
+        fused = jnp.minimum(steps, p1 - p0 - first_steps)
+
+        def first_step(s, fetch):
+            wait_first(first, first_sem, s)
             wait_piece(p0 + s)
+            if fetch:
+                start_items(cache, more, more_sem, s)
             attend_step(s, False)
             piece(p0 + s)
-            refill(cache, ring, sem, s)
             after_piece(p0 + s)
 
-        fused = jnp.minimum(steps, p1 - p0)
-
-        @pl.loop(first_steps, fused)
+        @pl.loop(0, fetching)
         def _(s):
-            wait_step(ring, sem, s)
-            wait_piece(p0 + s)
+            first_step(s, True)
+
+        @pl.loop(fetching, first_steps)
+        def _(s):
+            first_step(s, False)
+
+        @pl.loop(0, fused)
+        def _(s):
+            wait_more(more, more_sem, s)
+            wait_piece(p0 + first_steps + s)
             attend_step(s, True)
-            piece(p0 + s)
-            refill(cache, ring, sem, s)
-            after_piece(p0 + s)
+            piece(p0 + first_steps + s)
+            refill(cache, more, more_sem, s)
+            after_piece(p0 + first_steps + s)
 
         @pl.loop(fused, steps)
         def _(s):
-            wait_step(ring, sem, s)
+            wait_more(more, more_sem, s)
             attend_step(s, True)
-            refill(cache, ring, sem, s)
-
-        return p0 + fused
-
-    reached = both(score_step, k_cache, k_ring, k_sem, 0, PIECES_SCORE)
+            refill(cache, more, more_sem, s)
+
+        return p0 + first_steps + fused
+
+    reached = both(score_step, k_cache, k_first, kf_sem, k_more, km_sem, 0, PIECES_SCORE)
 
     @pl.loop(reached, PIECES_SCORE)
     def _(p):
@@ -283,7 +298,7 @@
         o = jnp.dot(p.reshape(CHUNK * sub, lanes).astype(BF16), vn_buf[:, rows].reshape(lanes, head_dim), preferred_element_type=F32)
         mixed[rows] = o.reshape(CHUNK, sub, head_dim)
 
-    reached = both(value_step, v_cache, v_ring, v_sem, PIECES_SCORE, PIECES_SCORE + PIECES_VALUE)
+    reached = both(value_step, v_cache, v_first, vf_sem, v_more, vm_sem, PIECES_SCORE, PIECES_SCORE + PIECES_VALUE)
 
     q_buf[...] = mixed[:batch] / jnp.sum(total[:batch], axis=-1, keepdims=True)
     for h in range(heads):
@@ -312,7 +327,7 @@
     width = w_gate.shape[1]
     half_freq = np.exp(np.arange(head_dim // 2) * (-2.0 * math.log(ROPE_BASE) / head_dim))
     freq = jnp.asarray(np.concatenate([half_freq, half_freq])[None, :], F32)
-    items = batch * (context // CHUNK) + UNROLL
+    items = batch * (context // CHUNK) + 2 * UNROLL
     lanes = local_kv * CHUNK
     dma = pltpu.SemaphoreType.DMA
     hbm = pl.BlockSpec(memory_space=pltpu.HBM)
@@ -326,6 +341,8 @@
             pltpu.VMEM((batch, model_dim), BF16),
             pltpu.VMEM((batch, model_dim), BF16),
             pltpu.VMEM((SLOTS, model_dim, TILE), BF16),
+            pltpu.VMEM((batch, local_kv, CHUNK, head_dim), BF16),
+            pltpu.VMEM((batch, local_kv, CHUNK, head_dim), BF16),
             pltpu.VMEM((RING, local_kv, CHUNK, head_dim), BF16),
             pltpu.VMEM((RING, local_kv, CHUNK, head_dim), BF16),
             pltpu.VMEM((batch, 8, head_dim), F32),
@@ -345,7 +362,8 @@
             pltpu.VMEM((batch, width), BF16),
             pltpu.SMEM((items,), jnp.int32),
             pltpu.SMEM((items,), jnp.int32),
-            dma((7,)), dma((3,)), dma((SLOTS,)), dma((RING // UNROLL,)), dma((RING // UNROLL,)),
+            dma((7,)), dma((3,)), dma((SLOTS,)), dma((batch // UNROLL,)), dma((batch // UNROLL,)),
+            dma((RING // UNROLL,)), dma((RING // UNROLL,)),
         ],
         compiler_params=pltpu.CompilerParams(vmem_limit_bytes=VMEM_BYTES),
         name="front",

time: 49.4 us -> 47.6 us (0.964)
  Pallas kernels: 48.7 us -> 46.9 us
    pallas_call x1, Pallas kernels: 25.1 us -> 23.3 us  [front(): pl.pallas_call(front_kernel, out_shape=jax.ShapeDtypeStruct((batch, width...]
where the time goes in v2:
time: 47.6 us; the launch traced here: 47.5 us
  Pallas kernels  46.9 us (99%)
  between operations  0.65 us (1%)
    pallas_call x1, Pallas kernels, front(): pl.pallas_call(front_kernel, out_shape=jax.ShapeDtypeStruct((batch, width...  23.3 us
    pallas_call x1, Pallas kernels, back(): pl.pallas_call(back_kernel, out_shape=(jax.ShapeDtypeStruct((devices, row...  22.6 us

profile of v2, /device:TPU:0, one launch (start us, length us, event | category | flops | bytes accessed | tf_op | source)
XLA Modules:
  0.0 47.5 jit_solution(10125617346772830806)
XLA Ops:
  0.6 23.3 %front.1.packed = bf16[128,5120]{1,0:T(8,128)(2,1)} custom-call(s32[128]{0:T(128)} %lengths.1, bf16[128,3072]{1,0:T(8,128)(2,1)} %tokens.1, bf16[3072]{0:T(1024)(128)(2,1)} %gain_hbm.1, f32[1,128]{1,0:T(1,128)} %constant.2.clone.freq_hbm, bf16[128,8,512,128]{3,2,1,0:T(8,128)(2,1)} %k_cache.1, bf16[128,8,512,128]{3,2,1,0:T(8,128)(2,1)} %v_cache.1, ...), custom_call_target="tpu_custom_call" | custom-call | tf_op jit(solution)/shard_map/front/pallas_call | solution.py:335
  24.0 22.6 %back.1 = (bf16[4,32,3072]{2,1,0:T(8,128)(2,1)S(1)}, bf16[32,8,128]{2,1,0:T(8,128)(2,1)S(1)}, bf16[32,8,128]{2,1,0:T(8,128)(2,1)S(1)}, bf16[128,5120]{1,0:T(8,128)(2,1)}) custom-call(bf16[128,5120]{1,0:T(8,128)(2,1)} %front.1.packed, bf16[3072,3072]{1,0:T(8,128)(2,1)} %w_down.1, bf16[768,3072]{1,0:T(8,128)(2,1)} %w_out.1), custom_call_target="tpu_custom_call", output_to_operand_aliasing={{3}: (0, {})} | custom-call | tf_op jit(solution)/shard_map/back/pallas_call | solution.py:529
  46.6 0.9 %finish.1 = (bf16[128,3072]{1,0:T(8,128)(2,1)}, bf16[32,8,128]{2,1,0:T(8,128)(2,1)}, bf16[32,8,128]{2,1,0:T(8,128)(2,1)}) custom-call(bf16[128,3072]{1,0:T(8,128)(2,1)S(1)} %bitcast.1, bf16[32,8,128]{2,1,0:T(8,128)(2,1)S(1)} %get-tuple-element.7.refs_1_, bf16[32,8,128]{2,1,0:T(8,128)(2,1)S(1)} %get-tuple-element.8.refs_2_), custom_call_target="tpu_custom_call" | custom-call | tf_op jit(solution)/shard_map/finish/pallas_call | solution.py:570

commit v3 on v2

--- a/solution.py
+++ b/solution.py
@@ -451,13 +451,15 @@
         total += jnp.dot(u_buf[...], w_buf[c], preferred_element_type=F32)
         part[c] = total.reshape(part.shape[1:])
 
-    product(0)
-    for copy in (*kv_copies, *x_copies):
+    for copy in kv_copies:
         copy.wait()
     pl.semaphore_wait(barrier, 3)
-    sib_send(0).start()
     for n in range(3):
         kv_copy(n).start()
+    product(0)
+    sib_send(0).start()
+    for copy in x_copies:
+        copy.wait()
 
     @pl.loop(1, n_out + lag_store)
     def _(i):

time: 47.6 us -> 47.9 us (level)
  no operation moved by 1% of the time
where the time goes in v3:
time: 47.9 us; the launch traced here: 47.5 us
  Pallas kernels  46.8 us (98%)
  between operations  0.65 us (1%)
    pallas_call x1, Pallas kernels, front(): pl.pallas_call(front_kernel, out_shape=jax.ShapeDtypeStruct((batch, width...  23.3 us
    pallas_call x1, Pallas kernels, back(): pl.pallas_call(back_kernel, out_shape=(jax.ShapeDtypeStruct((devices, row...  22.6 us

profile of v3, /device:TPU:0, one launch (start us, length us, event | category | flops | bytes accessed | tf_op | source)
XLA Modules:
  0.0 47.5 jit_solution(13798454987276030462)
XLA Ops:
  0.6 23.3 %front.1.packed = bf16[128,5120]{1,0:T(8,128)(2,1)} custom-call(s32[128]{0:T(128)} %lengths.1, bf16[128,3072]{1,0:T(8,128)(2,1)} %tokens.1, bf16[3072]{0:T(1024)(128)(2,1)} %gain_hbm.1, f32[1,128]{1,0:T(1,128)} %constant.2.clone.freq_hbm, bf16[128,8,512,128]{3,2,1,0:T(8,128)(2,1)} %k_cache.1, bf16[128,8,512,128]{3,2,1,0:T(8,128)(2,1)} %v_cache.1, ...), custom_call_target="tpu_custom_call" | custom-call | tf_op jit(solution)/shard_map/front/pallas_call | solution.py:335
  23.9 22.6 %back.1 = (bf16[4,32,3072]{2,1,0:T(8,128)(2,1)S(1)}, bf16[32,8,128]{2,1,0:T(8,128)(2,1)S(1)}, bf16[32,8,128]{2,1,0:T(8,128)(2,1)S(1)}, bf16[128,5120]{1,0:T(8,128)(2,1)}) custom-call(bf16[128,5120]{1,0:T(8,128)(2,1)} %front.1.packed, bf16[3072,3072]{1,0:T(8,128)(2,1)} %w_down.1, bf16[768,3072]{1,0:T(8,128)(2,1)} %w_out.1), custom_call_target="tpu_custom_call", output_to_operand_aliasing={{3}: (0, {})} | custom-call | tf_op jit(solution)/shard_map/back/pallas_call | solution.py:531
  46.6 0.9 %finish.1 = (bf16[128,3072]{1,0:T(8,128)(2,1)}, bf16[32,8,128]{2,1,0:T(8,128)(2,1)}, bf16[32,8,128]{2,1,0:T(8,128)(2,1)}) custom-call(bf16[128,3072]{1,0:T(8,128)(2,1)S(1)} %bitcast.1, bf16[32,8,128]{2,1,0:T(8,128)(2,1)S(1)} %get-tuple-element.7.refs_1_, bf16[32,8,128]{2,1,0:T(8,128)(2,1)S(1)} %get-tuple-element.8.refs_2_), custom_call_target="tpu_custom_call" | custom-call | tf_op jit(solution)/shard_map/finish/pallas_call | solution.py:572
